TPU v7x, 32 devices: a whole 2x2x4 slice. The times are simulated.
32 devices in a mesh: expert: 4 (over z), neuron: 8 (over y, x, core).
Axes of the slice: x: 2, y: 2, z: 4, core: 2. Of those that a mesh axis runs over, the one named last changes fastest.
Arguments:
- tokens: bfloat16 [256, 4096], P('neuron'), may hold values from -6 to 6
- route_logits: float32 [256, 2], replicated, may hold values from -6 to 6
- expert_ids: int32 [256, 2], replicated, may hold values from 0 to 3, all different within a row; in each aligned block of 256 rows (0 to 255, 256 to 511, ...) at most 128 rows name the same one
- block_live: int32 [4, 224], P('expert', 'neuron'), may hold values 0 or 1
- w_gate: bfloat16 [4, 4096, 14336], P('expert', None, 'neuron'), may hold values from -0.09375 to 0.09375
- w_up: bfloat16 [4, 4096, 14336], P('expert', None, 'neuron'), may hold values from -0.09375 to 0.09375
- w_down: bfloat16 [4, 14336, 4096], P('expert', 'neuron'), may hold values from -0.046875 to 0.046875
Outputs:
- mixed: bfloat16 [256, 4096], P('neuron')
Inputs may be any that keep to these rules, and one draw needn't show every extreme that they name: `expert_ids`: each token names two different experts; no expert is named by more than 128 tokens, a bound that some block reaches; every expert is named.
All inputs are finite; a program needn't handle non-finite values. No bound on the sum of `block_live` on one device may be relied on, other than what follows from the above.
Results may differ from a plain program's by a relative error of at most 0.0049.
Values may be sent and summed in bfloat16 or wider, within the bound.
A program may use at most 128 MiB of HBM per device.

v0:
```python
import jax
import jax.numpy as jnp
from jax import lax
from jax.sharding import PartitionSpec as P

BLK = 64


def routing(expert_ids, route_logits, expert, capacity):
    chosen = (expert_ids == expert).astype(jnp.int32)
    flat_hits = chosen.reshape(-1)
    before = (jnp.cumsum(flat_hits) - flat_hits).reshape(chosen.shape)
    slot_pair = jnp.where(chosen > 0, before, capacity)
    leading = jax.nn.sigmoid(route_logits[:, 0] - route_logits[:, 1])
    mix_gates = jnp.stack([leading, 1.0 - leading], axis=1)
    weight = jnp.sum(mix_gates * chosen.astype(jnp.float32), axis=1)
    slot_tok = jnp.min(slot_pair, axis=1)
    slot_index = lax.broadcasted_iota(jnp.int32, (capacity, expert_ids.shape[0]), 0)
    dispatch = (
        (slot_pair[None, :, 0] == slot_index) | (slot_pair[None, :, 1] == slot_index)
    ).astype(jnp.bfloat16)
    return (dispatch, slot_tok, weight)


def per_device(tokens, route_logits, expert_ids, block_live, w_gate, w_up, w_down):
    total_tokens = expert_ids.shape[0]
    capacity = total_tokens // 2
    expert = lax.axis_index("expert")
    dispatch, slot_tok, weight = routing(expert_ids, route_logits, expert, capacity)
    gathered = jnp.dot(
        dispatch,
        lax.all_gather(tokens, "neuron", axis=0, tiled=True),
        preferred_element_type=jnp.float32,
    ).astype(jnp.bfloat16)
    gate_val = jnp.dot(gathered, w_gate[0], preferred_element_type=jnp.float32)
    up_val = jnp.dot(gathered, w_up[0], preferred_element_type=jnp.float32)
    live = jnp.repeat(block_live[0].astype(jnp.float32), BLK)
    hidden = (jax.nn.silu(gate_val) * up_val * live[None, :]).astype(jnp.bfloat16)
    partial_value = jnp.dot(hidden, w_down[0], preferred_element_type=jnp.float32)
    picked = jnp.take(partial_value, jnp.minimum(slot_tok, capacity - 1), axis=0)
    weighted = weight[:, None] * picked
    own_part = lax.psum_scatter(weighted, "neuron", scatter_dimension=0, tiled=True)
    mixed = lax.psum(own_part, "expert")
    return mixed.astype(jnp.bfloat16)


def solution(mesh):
    placed = (
        P("neuron", None),
        P(),
        P(),
        P("expert", "neuron"),
        P("expert", None, "neuron"),
        P("expert", None, "neuron"),
        P("expert", "neuron", None),
    )
    return jax.shard_map(
        per_device, mesh=mesh, in_specs=placed, out_specs=P("neuron", None), check_vma=False
    )
```

profile of v0, /device:TPU:0, one launch (start us, length us, event | category | flops | bytes accessed | tf_op | source)
XLA Modules:
  0.0 162.3 jit_solution(13914430239259568634)
XLA Ops:
  6.5 0.0 all-gather.2.cloned.1.call-start
  6.5 0.7 all-gather.2.cloned.1.call-update
  7.3 0.0 reduce-scatter.2.cloned.1.call-start
  7.3 0.8 broadcast_subtract_fusion
  8.1 0.7 fusion.23
  8.8 0.1 copy.21
  8.9 0.1 reshape.51
  9.1 0.3 reduce-window.9
  9.4 0.1 slice.21
  9.5 0.1 reshape.52
  9.6 0.7 convert_bitcast_fusion
  10.3 0.1 broadcast_in_dim.20
  10.3 0.1 mul.32
  10.4 0.1 slice_reduce_fusion
  10.6 0.1 broadcast.55
  10.6 0.1 reshape.54
  10.7 0.1 copy.22
  10.9 28.9 %all-gather.2.cloned.1.call-done = bf16[256,4096]{1,0:T(8,128)(2,1)} async-done(((bf16[32,4096]{1,0:T(8,128)(2,1)}), bf16[256,4096]{1,0:T(8,128)(2,1)}) %all-gather.2.cloned.1.call-update) | async-done | bytes 2097168 | tf_op jit(solution)/shard_map/all_gather | solution.py:32
  39.8 2.0 %convolution_convert_fusion = bf16[128,4096]{1,0:T(8,128)(2,1)S(1)} fusion(bf16[256,4096]{1,0:T(8,128)(2,1)} %all-gather.2.cloned.1.call-done, s32[256]{0:T(256)S(1)} %bitcast.27, s32[256]{0:T(256)S(1)} %bitcast.26), kind=kOutput, calls=%fused_computation.7 | convolution fusion | flops 269058048 | bytes 3147776 | tf_op jit(solution)/shard_map/dot_general | solution.py:30
  41.8 8.2 %fusion.4 = f32[128,1792]{1,0:T(8,128)} fusion(bf16[128,4096]{1,0:T(8,128)(2,1)S(1)} %convolution_convert_fusion, bf16[1,4096,1792]{2,1,0:T(8,128)(2,1)} %param.11), kind=kOutput, calls=%fused_computation.5 | convolution fusion | flops 1879048192 | bytes 16646144 | tf_op jit(solution)/shard_map/dot_general | solution.py:35
  50.0 14.1 %fusion = f32[128,4096]{1,0:T(8,128)S(1)} fusion(bf16[1,1792,4096]{2,1,0:T(8,128)(2,1)} %param.13, bf16[128,4096]{1,0:T(8,128)(2,1)S(1)} %convolution_convert_fusion, bf16[1,4096,1792]{2,1,0:T(8,128)(2,1)} %param.12, f32[128,1792]{1,0:T(8,128)} %fusion.4, f32[1792]{0:T(1024)S(1)} %mul.32), kind=kOutput, calls=%fused_computation.1 | convolution fusion | flops 3759702016 | bytes 33430528 | tf_op jit(solution)/shard_map/dot_general | solution.py:39
  64.1 3.8 %gather_fusion = f32[256,4096]{1,0:T(8,128)} fusion(f32[128,4096]{1,0:T(8,128)S(1)} %fusion, s32[1024]{0:T(1024)S(1)} %pad_clamp_fusion), kind=kCustom, calls=%fused_computation | custom fusion | bytes 8389632 | tf_op jit(solution)/shard_map/jit(_take)/gather | solution.py:40
  67.9 4.9 %select_multiply_fusion = f32[256,4096]{1,0:T(8,128)} fusion(f32[256,4096]{1,0:T(8,128)} %gather_fusion, f32[256]{0:T(256)S(1)} %get-tuple-element.5, pred[256]{0:T(512)(128)(4,1)S(1)} %compare_and_fusion), kind=kLoop, calls=%fused_computation.8 | loop fusion | flops 2097152 | bytes 8389888 | tf_op jit(solution)/shard_map/mul | solution.py:41
  72.8 0.0 reduce-scatter.2.cloned.1.call-update
  72.8 51.3 %reduce-scatter.2.cloned.1.call-done = f32[32,4096]{1,0:T(8,128)} async-done(((f32[256,4096]{1,0:T(8,128)}), f32[32,4096]{1,0:T(8,128)}) %reduce-scatter.2.cloned.1.call-update) | async-done | bytes 524304 | tf_op jit(solution)/shard_map/reduce_scatter | solution.py:42
  124.1 31.4 %all-reduce.1 = bf16[32,4096]{1,0:T(8,128)(2,1)} all-reduce(f32[32,4096]{1,0:T(8,128)} %reduce-scatter.2.cloned.1.call-done), channel_id=1, replica_groups=mesh['expert'=4,'neuron'=8] {'expert'}, use_global_device_ids=true, to_apply=%region_5.6 | all-reduce | flops 131072 | bytes 786432 | tf_op jit(solution)/shard_map/psum | solution.py:43
  (7 shorter events, 0.1 us)
Async XLA Ops:
  6.5 33.2 %all-gather.2.cloned.1.call-start = ((), (), s32[]{:S(2)}) async-start(), calls=%async_computation.1 | async-start | bytes 2359296 | tf_op jit(solution)/shard_map/all_gather | solution.py:32
  7.3 116.8 %reduce-scatter.2.cloned.1.call-start = ((), (), s32[]{:S(2)}) async-start(), calls=%async_computation.2 | async-start | bytes 4718592 | tf_op jit(solution)/shard_map/reduce_scatter | solution.py:42
Sparse Core Ops, SparseCore 0:
  9.2 30.5 all-gather.1
  72.9 51.1 reduce-scatter.1
where the time goes:
time: 163 us; the launch traced here: 162 us
  waiting for transfers between devices  80.9 us (50%)
  blocking collectives  31.4 us (19%)
  matrix products  24.3 us (15%)
  between operations  13.5 us (8%)
  other arithmetic  7.42 us (5%)
  local copies, waits for them, and re-layouts  4.83 us (3%)
    reduce_scatter x1, waiting for transfers between devices, per_device(): lax.psum_scatter(weighted, 'neuron', scatter_dimension=0, tiled=True)  51.3 us
    psum x1, blocking collectives, per_device(): mixed = lax.psum(own_part, 'expert')  31.4 us
    all_gather x1, waiting for transfers between devices, per_device(): lax.all_gather(tokens, 'neuron', axis=0, tiled=True)  28.9 us
    dot_general x1, matrix products, per_device(): jnp.dot(hidden, w_down[0], preferred_element_type=jnp.float32)  14.1 us
    dot_general x1, matrix products, per_device(): gate_val = jnp.dot(gathered, w_gate[0], preferred_element_type=jnp.float32)  8.18 us
    mul x1, other arithmetic, per_device(): weighted = weight[:, None] * picked  4.89 us
    gather x1, local copies, waits for them, and re-layouts, per_device(): jnp.take(partial_value, jnp.minimum(slot_tok, capacity - 1), axis=0)  3.82 us
  transfers between devices with their start and end apart: 2, of which 2 were waited for; matrix products, arithmetic and copies ran while one was open for 2% of the time, Pallas kernels for 0%

commit v1 on v0

v1 whole, which is shorter than its diff:
```python
import functools

import jax
import jax.numpy as jnp
from jax import lax
from jax.experimental import pallas as pl
from jax.experimental.pallas import tpu as pltpu
from jax.sharding import PartitionSpec as P

GROUPS = 4
TILE = 256
F32, BF16 = jnp.float32, jnp.bfloat16


def flipped(me, bit):
    return me + (1 - 2 * ((me // (1 << bit)) % 2)) * (1 << bit)


def bit_orders(bits):
    rest = list(range(1, bits))
    return ([0] + rest, [0] + rest[::-1])


def kernel(
    experts, neurons,
    ids_ref, logits_ref, live_ref, tok_hbm, wg_hbm, wu_hbm, wd_hbm,
    out_ref,
    wg, wu, wd, tb, xg, gate, up, hid, sb, rb, eb, fin, comb, combs, disps, sw, live,
    w_sem, t_sem, ag_s, ag_r, rs_s, rs_r, xr_s, xr_r, xa_s, xa_r,
):
    e = lax.axis_index("expert")
    me = lax.axis_index("neuron")
    bits = neurons.bit_length() - 1
    orders = bit_orders(bits)
    total, _ = ids_ref.shape
    rows, width = tok_hbm.shape
    capacity = total // 2
    cols = width // GROUPS
    part = cols // experts
    inner = wg.shape[1]
    tile = TILE if inner % TILE == 0 else inner
    out_tile = TILE if cols % TILE == 0 else cols

    tok_in = []
    for g in range(GROUPS):
        c = pltpu.make_async_copy(
            tok_hbm.at[:, pl.ds(g * cols, cols)], tb.at[g, pl.ds(0, rows)], t_sem.at[g])
        c.start()
        tok_in.append(c)
    up_in, down_in = [], []
    for g in range(GROUPS):
        k = pl.ds(g * cols, cols)
        pair = (pltpu.make_async_copy(wg_hbm.at[0, k], wg.at[k], w_sem.at[0, g]),
                pltpu.make_async_copy(wu_hbm.at[0, k], wu.at[k], w_sem.at[1, g]))
        for c in pair:
            c.start()
        up_in.append(pair)
    for g in range(GROUPS):
        c = pltpu.make_async_copy(wd_hbm.at[0, :, pl.ds(g * cols, cols)], wd.at[g], w_sem.at[2, g])
        c.start()
        down_in.append(c)

    barrier = pltpu.get_barrier_semaphore()
    for b in range(bits):
        pl.semaphore_signal(barrier, inc=1, device_id={"neuron": flipped(me, b)})
    for j in range(1, experts):
        pl.semaphore_signal(barrier, inc=1, device_id={"expert": (e + j) % experts})
    pl.semaphore_wait(barrier, bits + experts - 1)

    def gather_copy(g, step):
        count = rows << step
        bit = orders[g % 2][bits - 1 - step]
        return pltpu.make_async_remote_copy(
            src_ref=tb.at[g, pl.ds(0, count)], dst_ref=tb.at[g, pl.ds(count, count)],
            send_sem=ag_s.at[g, step], recv_sem=ag_r.at[g, step],
            device_id={"neuron": flipped(me, bit)})

    gathers = [[gather_copy(g, s) for s in range(bits)] for g in range(GROUPS)]
    for g in range(GROUPS):
        tok_in[g].wait()
        gathers[g][0].start()

    ids = ids_ref[...]
    logits = logits_ref[...]
    first, second = ids[:, 0:1] == e, ids[:, 1:2] == e
    chosen = jnp.where(first | second, 1.0, 0.0).astype(F32)
    leading = 1.0 / (1.0 + jnp.exp(logits[:, 1:2] - logits[:, 0:1]))
    weight = jnp.where(first, leading, 0.0) + jnp.where(second, 1.0 - leading, 0.0)
    tri = jnp.where(
        lax.broadcasted_iota(jnp.int32, (total, total), 1)
        < lax.broadcasted_iota(jnp.int32, (total, total), 0), 1.0, 0.0).astype(BF16)
    chosen_wide = jnp.broadcast_to(chosen, (total, capacity))
    slot = jnp.dot(tri, chosen_wide.astype(BF16), preferred_element_type=F32)
    lane = lax.broadcasted_iota(jnp.int32, (total, capacity), 1).astype(F32)
    one_hot = jnp.where(slot == lane, chosen_wide, 0.0)
    comb[...] = one_hot
    sw[...] = jnp.sum((one_hot * weight).T, axis=1, keepdims=True)
    for o in range(2):
        for p in range(neurons):
            owner = me
            for place, bit in enumerate(orders[o]):
                if (p >> (bits - 1 - place)) & 1:
                    owner = owner + (1 - 2 * ((me // (1 << bit)) % 2)) * (1 << bit)
            block = comb[pl.ds(pl.multiple_of(owner * rows, rows), rows), :]
            combs[o, pl.ds(p * rows, rows), :] = block.astype(BF16)
        disps[o] = combs[o].astype(F32).T.astype(BF16)

    blocks = live_ref.shape[1]
    number = lax.broadcasted_iota(jnp.int32, (8, inner), 1) // (inner // blocks)
    kept = jnp.zeros((8, inner), jnp.int32)
    for b in range(blocks):
        kept = jnp.where(number == b, live_ref[0, b], kept)
    live[...] = kept.astype(F32)

    def forward(g, step):
        gathers[g][step].wait_recv()
        if step + 1 < bits:
            gathers[g][step + 1].start()

    def gate_up(g):
        forward(g, bits - 1)
        xg[...] = jnp.dot(disps[g % 2], tb[g], preferred_element_type=F32).astype(BF16)
        for c in up_in[g]:
            c.wait()
        k = pl.ds(g * cols, cols)

        def body(i, carry):
            n = pl.ds(pl.multiple_of(i * tile, 128), tile) if inner > tile else pl.ds(0, tile)
            gv = jnp.dot(xg[...], wg[k, n], preferred_element_type=F32)
            uv = jnp.dot(xg[...], wu[k, n], preferred_element_type=F32)
            if g > 0:
                gv, uv = gv + gate[:, n], uv + up[:, n]
            if g < GROUPS - 1:
                gate[:, n] = gv
                up[:, n] = uv
            else:
                hid[:, n] = (gv / (1.0 + jnp.exp(-gv)) * uv * live[0:1, n]).astype(BF16)
            return carry

        lax.fori_loop(0, inner // tile, body, 0)

    for step in range(bits - 2):
        for g in range(GROUPS):
            forward(g, step)
    for lo in range(0, GROUPS, 2):
        for g in (lo, lo + 1):
            forward(g, bits - 2)
        for g in (lo, lo + 1):
            gate_up(g)

    def scatter_copy(g, step):
        half = total >> (step + 1)
        here = pl.ds(half, half)
        return pltpu.make_async_remote_copy(
            src_ref=sb.at[g, here], dst_ref=rb.at[g, here],
            send_sem=rs_s.at[g, step], recv_sem=rs_r.at[g, step],
            device_id={"neuron": flipped(me, orders[g % 2][step])})

    def peer_columns(g, who, base):
        return pl.ds(pl.multiple_of(base + who * part, 128), part)

    def combine_copy(g, j):
        who = (e + j) % experts
        return pltpu.make_async_remote_copy(
            src_ref=sb.at[g, pl.ds(0, rows), peer_columns(g, who, 0)], dst_ref=eb.at[g, j - 1],
            send_sem=xr_s.at[g, j - 1], recv_sem=xr_r.at[g, j - 1],
            device_id={"expert": who})

    def spread_copy(g, j):
        mine = fin.at[:, peer_columns(g, e, g * cols)]
        return pltpu.make_async_remote_copy(
            src_ref=mine, dst_ref=mine,
            send_sem=xa_s.at[g, j - 1], recv_sem=xa_r.at[g, j - 1],
            device_id={"expert": (e + j) % experts})

    scatters = [[scatter_copy(g, s) for s in range(bits)] for g in range(GROUPS)]
    combines = [[combine_copy(g, j) for j in range(1, experts)] for g in range(GROUPS)]
    spreads = [[spread_copy(g, j) for j in range(1, experts)] for g in range(GROUPS)]

    def down(g):
        down_in[g].wait()

        def body(i, carry):
            n = pl.ds(pl.multiple_of(i * out_tile, 128), out_tile)
            value = jnp.dot(hid[...], wd[g, :, n], preferred_element_type=F32)
            value = (value * sw[...]).astype(BF16)
            sb[g, :, n] = jnp.dot(combs[g % 2], value, preferred_element_type=F32).astype(BF16)
            return carry

        lax.fori_loop(0, cols // out_tile, body, 0)
        scatters[g][0].start()

    def reduce(g, step):
        half = total >> (step + 1)
        scatters[g][step].wait_recv()
        sb[g, pl.ds(0, half), :] = (
            sb[g, pl.ds(0, half), :].astype(F32) + rb[g, pl.ds(half, half), :].astype(F32)
        ).astype(BF16)
        if step + 1 < bits:
            scatters[g][step + 1].start()
        else:
            for c in combines[g]:
                c.start()

    def combine(g):
        value = sb[g, pl.ds(0, rows), peer_columns(g, e, 0)].astype(F32)
        for j, c in enumerate(combines[g]):
            c.wait_recv()
            value = value + eb[g, j].astype(F32)
        fin[:, peer_columns(g, e, g * cols)] = value.astype(BF16)
        for c in spreads[g]:
            c.start()

    for slot_no in range(GROUPS + bits + 1):
        if slot_no < GROUPS:
            down(slot_no)
        for g in range(GROUPS):
            stage = slot_no - g - 1
            if 0 <= stage < bits:
                reduce(g, stage)
            elif stage == bits:
                combine(g)

    for g in range(GROUPS):
        for c in spreads[g]:
            c.wait_recv()
    out_ref[...] = fin[...]
    for group in (gathers, scatters, combines, spreads):
        for copies in group:
            for c in copies:
                c.wait_send()


def per_device(experts, neurons, tokens, route_logits, expert_ids, block_live, w_gate, w_up, w_down):
    total = expert_ids.shape[0]
    rows, width = tokens.shape
    capacity = total // 2
    inner = w_gate.shape[2]
    cols = width // GROUPS
    bits = neurons.bit_length() - 1
    vmem = pl.BlockSpec(memory_space=pltpu.VMEM)
    hbm = pl.BlockSpec(memory_space=pl.ANY)
    dma = pltpu.SemaphoreType.DMA
    return pl.pallas_call(
        functools.partial(kernel, experts, neurons),
        out_shape=jax.ShapeDtypeStruct((rows, width), BF16),
        in_specs=[vmem, vmem, pl.BlockSpec(memory_space=pltpu.SMEM), hbm, hbm, hbm, hbm],
        out_specs=vmem,
        scratch_shapes=[
            pltpu.VMEM((width, inner), BF16),
            pltpu.VMEM((width, inner), BF16),
            pltpu.VMEM((GROUPS, inner, cols), BF16),
            pltpu.VMEM((GROUPS, total, cols), BF16),
            pltpu.VMEM((capacity, cols), BF16),
            pltpu.VMEM((capacity, inner), F32),
            pltpu.VMEM((capacity, inner), F32),
            pltpu.VMEM((capacity, inner), BF16),
            pltpu.VMEM((GROUPS, total, cols), BF16),
            pltpu.VMEM((GROUPS, total, cols), BF16),
            pltpu.VMEM((GROUPS, experts - 1, rows, cols // experts), BF16),
            pltpu.VMEM((rows, width), BF16),
            pltpu.VMEM((total, capacity), F32),
            pltpu.VMEM((2, total, capacity), BF16),
            pltpu.VMEM((2, capacity, total), BF16),
            pltpu.VMEM((capacity, 1), F32),
            pltpu.VMEM((8, inner), F32),
            dma((3, GROUPS)), dma((GROUPS,)),
            dma((GROUPS, bits)), dma((GROUPS, bits)),
            dma((GROUPS, bits)), dma((GROUPS, bits)),
            dma((GROUPS, experts - 1)), dma((GROUPS, experts - 1)),
            dma((GROUPS, experts - 1)), dma((GROUPS, experts - 1)),
        ],
        compiler_params=pltpu.CompilerParams(
            collective_id=0, has_side_effects=True, vmem_limit_bytes=67043328),
    )(expert_ids, route_logits, block_live, tokens, w_gate, w_up, w_down)


def solution(mesh):
    placed = (
        P("neuron", None),
        P(),
        P(),
        P("expert", "neuron"),
        P("expert", None, "neuron"),
        P("expert", None, "neuron"),
        P("expert", "neuron", None),
    )
    body = functools.partial(per_device, mesh.shape["expert"], mesh.shape["neuron"])
    return jax.shard_map(
        body, mesh=mesh, in_specs=placed, out_specs=P("neuron", None), check_vma=False
    )
```

time: 163 us -> 77 us (0.47)
  waiting for transfers between devices: 80.9 us -> 0 us
  Pallas kernels: 0 us -> 72.2 us
  blocking collectives: 31.4 us -> 0 us
  matrix products: 24.3 us -> 0 us
  between operations: 13.5 us -> 0.01 us
  other arithmetic: 7.42 us -> 0 us
    pallas_call x0 -> x1, Pallas kernels: none -> 72.2 us  [per_device(): pl.pallas_call(functools.partial(kernel, experts, neurons), out_shape=jax...]
    reduce_scatter x1 -> x0, waiting for transfers between devices: 51.3 us -> none  [per_device(): lax.psum_scatter(weighted, 'neuron', scatter_dimension=0, tiled=True)]
    psum x1 -> x0, blocking collectives: 31.4 us -> none  [per_device(): mixed = lax.psum(own_part, 'expert')]
    all_gather x1 -> x0, waiting for transfers between devices: 28.9 us -> none  [per_device(): lax.all_gather(tokens, 'neuron', axis=0, tiled=True)]
    dot_general x3 -> x0, matrix products: 24.3 us -> none  [the longest x1 14.1 us: per_device(): jnp.dot(hidden, w_down[0], preferred_element_type=jnp.float32)]
    mul x1 -> x0, other arithmetic: 4.89 us -> none  [per_device(): weighted = weight[:, None] * picked]
    unnamed x0 -> x3, local copies, waits for them, and re-layouts: none -> 4.62 us
    gather x1 -> x0, local copies, waits for them, and re-layouts: 3.82 us -> none  [per_device(): jnp.take(partial_value, jnp.minimum(slot_tok, capacity - 1), axis=0)]
  transfers between devices with their start and end apart: 2 -> 0, of which waited for: 2 -> 0; matrix products, arithmetic and copies ran while one was open for 2% -> 0% of each run, Pallas kernels for 0% -> 0%
where the time goes in v1:
time: 77 us; the launch traced here: 76.8 us
  Pallas kernels  72.2 us (94%)
  local copies, waits for them, and re-layouts  4.62 us (6%)
    pallas_call x1, Pallas kernels, per_device(): pl.pallas_call(functools.partial(kernel, experts, neurons), out_shape=jax...  72.2 us
    unnamed x3, local copies, waits for them, and re-layouts  4.62 us

profile of v1, /device:TPU:0, one launch (start us, length us, event | category | flops | bytes accessed | tf_op | source)
XLA Modules:
  0.0 76.8 jit_solution(2240167851262350673)
XLA Ops:
  0.0 1.5 %copy.9.logits_ref = f32[256,2]{1,0:T(8,128)} copy(f32[256,2]{0,1:T(2,128)} %param.8) | data formatting | bytes 4096 | tf_op args[1]
  1.5 1.5 %copy.8.ids_ref = s32[256,2]{1,0:T(8,128)} copy(s32[256,2]{0,1:T(2,128)} %param.9) | data formatting | bytes 4096 | tf_op args[2]
  3.0 72.2 %shard_map.73 = bf16[32,4096]{1,0:T(8,128)(2,1)} custom-call(s32[256,2]{1,0:T(8,128)} %copy.8.ids_ref, f32[256,2]{1,0:T(8,128)} %copy.9.logits_ref, s32[1,28]{1,0:T(1,128)} %live_ref.1, bf16[32,4096]{1,0:T(8,128)(2,1)} %tok_hbm.1, bf16[1,4096,1792]{2,1,0:T(8,128)(2,1)} %wg_hbm.1, bf16[1,4096,1792]{2,1,0:T(8,128)(2,1)} %wu_hbm.1, bf16[1,1792,4096]{2,1,0:T(8,128)(2,1)} %wd_hbm.1), custom_call_target="tpu_custom_call" | custom-call | tf_op jit(solution)/shard_map/pallas_call | solution.py:244
  75.2 1.7 %copy.11 = bf16[32,4096]{1,0:T(8,128)(2,1)} copy(bf16[32,4096]{1,0:T(8,128)(2,1)} %shard_map.73) | data formatting | bytes 524288
